TPU v7x, 32 devices: a whole 2x2x4 slice. The times are simulated.
32 devices in a mesh: gx: 16 (over z, x, core), gy: 2 (over y).
Axes of the slice: x: 2, y: 2, z: 4, core: 2. Of those that a mesh axis runs over, the one named last changes fastest.
Arguments:
- temp_adjoint: float32 [8, 256, 2048], P(None, 'gy', 'gx'), may hold values from -6 to 6
- height_adjoint: float32 [256, 2048], P('gy', 'gx'), may hold values from -6 to 6
- east_velocity: float32 [8, 256, 2048], P(None, 'gy', 'gx'), may hold values from -0.8 to 0.8
- north_velocity: float32 [8, 256, 2048], P(None, 'gy', 'gx'), may hold values from -0.8 to 0.8
- temp_store: float32 [8, 256, 2048], P(None, 'gy', 'gx'), may hold values from -4 to 4
- salt_store: float32 [8, 256, 2048], P(None, 'gy', 'gx'), may hold values from -4 to 4
- slot_map: int32 [16, 2, 8], P('gx', 'gy'), may hold values from 0 to 7, each once within a row
- land_mask: int32 [8, 256, 2048], P(None, 'gy', 'gx'), may hold values 0 or 1
- ocean_depth: float32 [256, 2048], P('gy', 'gx'), may hold values from 0.1 to 1
Outputs:
- temp_back: float32 [8, 256, 2048], P(None, 'gy', 'gx')
- salt_back: float32 [8, 256, 2048], P(None, 'gy', 'gx')
- surface_adjoint: float32 [256, 2048], P('gy', 'gx')
Inputs may be any that keep to these rules, and one draw needn't show every extreme that they name: `slot_map`: each tile's entries over the last dimension name every slot 0 to 7 once.
All inputs are finite; a program needn't handle non-finite values. No bound on the sum of `land_mask` on one device may be relied on, other than what follows from the above.
Results may differ from a plain program's by a relative error of at most 0.00013.
Values sent between devices are 32-bit elements; how exact they have to be, the bound alone decides.
No kernel may reach another device: no remote copies, remote signals or barrier semaphores. Data moves between devices by JAX's collectives and lax.ppermute only.
A program may use at most 64 MiB of HBM per device.

v0:
```python
import jax
import jax.numpy as jnp
from jax import lax
from jax.sharding import PartitionSpec as P

ITERS = 6
DIFFUSE = 0.2
TIMESTEP = 1.0
STIFFNESS = 8.0
GRAVITY = 4.0
THERMAL = 0.5
NONLINEAR = 0.4
CABBELING = 0.3
HALINE = 0.8


def padded_2(block, sides, width):
    for axis, dim in sides:
        count = lax.axis_size(axis)
        forward = [(i, i + 1) for i in range(count - 1)]
        forward.append((count - 1, 0))
        backward = [(target, source) for source, target in forward]
        low = lax.ppermute(
            lax.slice_in_dim(block, block.shape[dim] - width, None, axis=dim), axis, forward
        )
        high = lax.ppermute(lax.slice_in_dim(block, 0, width, axis=dim), axis, backward)
        block = jnp.concatenate([low, block, high], axis=dim)
    return block


def shifted(value, axis, steps):
    count = lax.axis_size(axis)
    pairs = [(source, (source + steps) % count) for source in range(count)]
    return lax.ppermute(value, axis, pairs)


def clear_walls(padded, row_axis):
    row_index = lax.broadcasted_iota(jnp.int32, padded.shape, row_axis)
    row_count = padded.shape[row_axis]
    lower_wall = (row_index == 0) & (lax.axis_index("gy") == 0)
    upper_wall = (row_index == row_count - 1) & (lax.axis_index("gy") == lax.axis_size("gy") - 1)
    return jnp.where(lower_wall | upper_wall, jnp.zeros_like(padded), padded)


def side_cells(padded):
    return (
        padded[..., 1:-1, :-2],
        padded[..., 1:-1, 2:],
        padded[..., :-2, 1:-1],
        padded[..., 2:, 1:-1],
    )


def surface_apply(grid_field, face_weights):
    padded = padded_2(grid_field, (("gx", 1), ("gy", 0)), 1)
    applied = grid_field
    for face_weight, nearby in zip(face_weights, side_cells(padded)):
        applied = applied + face_weight * (grid_field - nearby)
    return applied


def paired(residual, image_field):
    return lax.psum((jnp.sum(residual * residual), jnp.sum(residual * image_field)), ("gx", "gy"))


def body(
    temp_adjoint,
    height_adjoint,
    east_velocity,
    north_velocity,
    temp_store,
    salt_store,
    slot_map,
    land_mask,
    ocean_depth,
):
    half_cycle = lax.axis_size("gx") // 2
    slot_order = slot_map.reshape(-1)
    both_states = jnp.take(jnp.stack((temp_store, salt_store)), slot_order, axis=1)
    fetched = shifted(both_states, "gx", half_cycle)
    wet_cells = land_mask.astype(jnp.float32)
    masked = wet_cells * temp_adjoint
    east_coef = DIFFUSE - 0.5 * east_velocity
    west_coef = DIFFUSE + 0.5 * east_velocity
    north_coef = DIFFUSE - 0.5 * north_velocity
    south_coef = DIFFUSE + 0.5 * north_velocity
    stacked = jnp.stack((masked, east_velocity, north_velocity))
    padded = padded_2(stacked, (("gx", 3), ("gy", 2)), 1)
    padded = clear_walls(padded, 2)
    mask_west, mask_east, mask_south, mask_north = side_cells(padded[0])
    speed_west, speed_east, _, _ = side_cells(padded[1])
    _, _, speed_south, speed_north = side_cells(padded[2])
    inflow = (DIFFUSE - 0.5 * speed_west) * mask_west + (DIFFUSE + 0.5 * speed_east) * mask_east
    inflow = (
        inflow
        + (DIFFUSE - 0.5 * speed_south) * mask_south
        + (DIFFUSE + 0.5 * speed_north) * mask_north
    )
    tracer_back = masked + TIMESTEP * (
        inflow - (east_coef + west_coef + north_coef + south_coef) * masked
    )
    open_cells = wet_cells[0]
    geometry = padded_2(jnp.stack((open_cells, ocean_depth)), (("gx", 2), ("gy", 1)), 1)
    geometry = clear_walls(geometry, 1)
    face_links = [open_cells * nearby for nearby in side_cells(geometry[0])]
    face_weights = [
        STIFFNESS * 0.5 * (ocean_depth + nearby) * link_open
        for nearby, link_open in zip(side_cells(geometry[1]), face_links)
    ]
    target = open_cells * height_adjoint
    solution = jnp.zeros_like(target)
    residual = target
    image_field = surface_apply(residual, face_weights)
    norm_now, product = paired(residual, image_field)
    step_size = norm_now / product
    direction = residual
    along_dir = image_field
    for iteration in range(ITERS):
        solution = solution + step_size * direction
        if iteration + 1 < ITERS:
            residual = residual - step_size * along_dir
            image_field = surface_apply(residual, face_weights)
            norm_next, product = paired(residual, image_field)
            growth = norm_next / norm_now
            step_size = norm_next / (product - growth * norm_next / step_size)
            direction = residual + growth * direction
            along_dir = image_field + growth * along_dir
            norm_now = norm_next
    height_load = ocean_depth * solution
    load_padded = padded_2(height_load, (("gx", 1), ("gy", 0)), 1)
    pressure_pull = jnp.zeros_like(height_load)
    for link_open, nearby in zip(face_links, side_cells(load_padded)):
        pressure_pull = pressure_pull + link_open * (nearby - height_load)
    adj_pressure = -GRAVITY * pressure_pull
    levels = temp_adjoint.shape[0]
    thickness = 1.0 + jnp.arange(levels, dtype=jnp.float32) / levels
    adj_density = thickness[:, None, None] * adj_pressure[None] * wet_cells
    ck_temp = fetched[0]
    ck_salt = fetched[1]
    temp_back = (
        tracer_back + (THERMAL + 2.0 * NONLINEAR * ck_temp + CABBELING * ck_salt) * adj_density
    )
    salt_back = (HALINE + CABBELING * ck_temp) * adj_density
    return (temp_back, salt_back, solution)


def solution(mesh):
    return jax.shard_map(
        body,
        mesh=mesh,
        in_specs=(
            P(None, "gy", "gx"),
            P("gy", "gx"),
            P(None, "gy", "gx"),
            P(None, "gy", "gx"),
            P(None, "gy", "gx"),
            P(None, "gy", "gx"),
            P("gx", "gy", None),
            P(None, "gy", "gx"),
            P("gy", "gx"),
        ),
        out_specs=(P(None, "gy", "gx"), P(None, "gy", "gx"), P("gy", "gx")),
        check_vma=False,
    )
```

profile of v0, /device:TPU:0, one launch (start us, length us, event | category | flops | bytes accessed | tf_op | source)
XLA Modules:
  0.0 398.7 jit_solution(17863209742963054110)
XLA Ops:
  3.5 5.0 %collective-permute-start.6 = (f32[2,128,1]{2,1,0:T(8,128)S(1)}, f32[2,128,1]{2,1,0:T(8,128)S(1)}, u32[]{:S(2)}, u32[]{:S(2)}) collective-permute-start(f32[2,128,1]{2,1,0:T(8,128)S(1)} %get-tuple-element.68), channel_id=1, source_target_pairs={{2,0},{4,2},{6,4},{8,6},{10,8},{12,10},{14,12},{16,14},{18,16},{20... | collective-permute-start | bytes 3080 | tf_op jit(solution)/shard_map/ppermute | solution.py:26
  9.3 1.9 collective-permute-done.5
  11.3 2.1 collective-permute-start.7
  13.4 2.3 collective-permute-done.9
  15.8 1.5 collective-permute-start.11
  18.1 1.3 collective-permute-done.11
  19.3 1.5 collective-permute-done.12
  21.7 37.1 %all-reduce.5 = (f32[]{:T(128)}, f32[]{:T(128)}) all-reduce(f32[]{:T(128)} %get-tuple-element.14, f32[]{:T(128)} %get-tuple-element.13), channel_id=1, replica_groups=mesh['gx'=16,'gy'=2] {'gx','gy'}, use_global_device_ids=true, to_apply=%region_1.2 | all-reduce | flops 2 | bytes 16 | tf_op jit(solution)/shard_map/psum | solution.py:63
  60.3 4.4 %collective-permute-start.14 = (f32[128,1]{1,0:T(8,128)S(1)}, f32[128,1]{1,0:T(8,128)S(1)}, u32[]{:S(2)}, u32[]{:S(2)}) collective-permute-start(f32[128,1]{1,0:T(8,128)S(1)} %get-tuple-element.80), channel_id=1, source_target_pairs={{2,0},{4,2},{6,4},{8,6},{10,8},{12,10},{14,12},{16,14},{18,16},{20... | collective-permute-start | bytes 1544 | tf_op jit(solution)/shard_map/ppermute | solution.py:26
  64.8 2.0 collective-permute-done.13
  66.9 2.4 collective-permute-start.15
  69.3 1.5 collective-permute-done.15
  70.8 2.0 collective-permute-done.16
  73.7 39.1 %all-reduce.4 = (f32[]{:T(128)}, f32[]{:T(128)}) all-reduce(f32[]{:T(128)} %get-tuple-element.12, f32[]{:T(128)} %get-tuple-element.11), channel_id=1, replica_groups=mesh['gx'=16,'gy'=2] {'gx','gy'}, use_global_device_ids=true, to_apply=%region_5.6 | all-reduce | flops 2 | bytes 16 | tf_op jit(solution)/shard_map/psum | solution.py:63
  117.5 4.4 %collective-permute-start.18 = (f32[128,1]{1,0:T(8,128)S(1)}, f32[128,1]{1,0:T(8,128)S(1)}, u32[]{:S(2)}, u32[]{:S(2)}) collective-permute-start(f32[128,1]{1,0:T(8,128)S(1)} %get-tuple-element.78), channel_id=1, source_target_pairs={{2,0},{4,2},{6,4},{8,6},{10,8},{12,10},{14,12},{16,14},{18,16},{20... | collective-permute-start | bytes 1544 | tf_op jit(solution)/shard_map/ppermute | solution.py:26
  122.0 2.0 collective-permute-done.17
  124.0 2.4 collective-permute-start.19
  126.7 1.3 collective-permute-done.19
  128.0 2.0 collective-permute-done.20
  130.8 37.5 %all-reduce.3 = (f32[]{:T(128)}, f32[]{:T(128)}) all-reduce(f32[]{:T(128)} %get-tuple-element.10, f32[]{:T(128)} %get-tuple-element.9), channel_id=1, replica_groups=mesh['gx'=16,'gy'=2] {'gx','gy'}, use_global_device_ids=true, to_apply=%region_9.10 | all-reduce | flops 2 | bytes 16 | tf_op jit(solution)/shard_map/psum | solution.py:63
  172.7 4.4 %collective-permute-start.22 = (f32[128,1]{1,0:T(8,128)}, f32[128,1]{1,0:T(8,128)S(1)}, u32[]{:S(2)}, u32[]{:S(2)}) collective-permute-start(f32[128,1]{1,0:T(8,128)} %get-tuple-element.76), channel_id=1, source_target_pairs={{2,0},{4,2},{6,4},{8,6},{10,8},{12,10},{14,12},{16,14},{18,16},{20... | collective-permute-start | bytes 1544 | tf_op jit(solution)/shard_map/ppermute | solution.py:26
  177.1 2.2 fusion.119
  179.3 2.0 copy.15
  181.8 4.4 %collective-permute-start.1 = (f32[3,8,128,1]{2,1,3,0:T(8,128)S(1)}, f32[3,8,128,1]{2,1,3,0:T(8,128)}, u32[]{:S(2)}, u32[]{:S(2)}) collective-permute-start(f32[3,8,128,1]{2,1,3,0:T(8,128)S(1)} %copy.16), channel_id=1, source_target_pairs={{2,0},{4,2},{6,4},{8,6},{10,8},{12,10},{14,12},{16,14},{18,16},{20... | collective-permute-start | bytes 36872 | tf_op jit(solution)/shard_map/ppermute | solution.py:26
  186.3 2.5 collective-permute-start.23
  188.9 1.5 collective-permute-done.23
  190.4 2.0 collective-permute-done.24
  192.4 1.7 multiply_reduce_fusion.3
  194.1 37.1 %all-reduce.2 = (f32[]{:T(128)}, f32[]{:T(128)}) all-reduce(f32[]{:T(128)} %get-tuple-element.8, f32[]{:T(128)} %get-tuple-element.7), channel_id=1, replica_groups=mesh['gx'=16,'gy'=2] {'gx','gy'}, use_global_device_ids=true, to_apply=%region_13.14 | all-reduce | flops 2 | bytes 16 | tf_op jit(solution)/shard_map/psum | solution.py:63
  235.2 4.4 %collective-permute-start.26 = (f32[128,1]{1,0:T(8,128)S(1)}, f32[128,1]{1,0:T(8,128)S(1)}, u32[]{:S(2)}, u32[]{:S(2)}) collective-permute-start(f32[128,1]{1,0:T(8,128)S(1)} %get-tuple-element.74), channel_id=1, source_target_pairs={{2,0},{4,2},{6,4},{8,6},{10,8},{12,10},{14,12},{16,14},{18,16},{20... | collective-permute-start | bytes 1544 | tf_op jit(solution)/shard_map/ppermute | solution.py:26
  239.6 2.0 collective-permute-done.25
  241.7 2.4 collective-permute-start.27
  244.3 1.3 pad_maximum_fusion.1
  245.7 2.0 collective-permute-done.28
  248.6 39.1 %all-reduce.1 = (f32[]{:T(128)}, f32[]{:T(128)}) all-reduce(f32[]{:T(128)} %get-tuple-element.6, f32[]{:T(128)} %get-tuple-element.5), channel_id=1, replica_groups=mesh['gx'=16,'gy'=2] {'gx','gy'}, use_global_device_ids=true, to_apply=%region_17.18 | all-reduce | flops 2 | bytes 16 | tf_op jit(solution)/shard_map/psum | solution.py:63
  291.9 4.4 %collective-permute-start.30 = (f32[128,1]{1,0:T(8,128)S(1)}, f32[128,1]{1,0:T(8,128)S(1)}, u32[]{:S(2)}, u32[]{:S(2)}) collective-permute-start(f32[128,1]{1,0:T(8,128)S(1)} %get-tuple-element.72), channel_id=1, source_target_pairs={{2,0},{4,2},{6,4},{8,6},{10,8},{12,10},{14,12},{16,14},{18,16},{20... | collective-permute-start | bytes 1544 | tf_op jit(solution)/shard_map/ppermute | solution.py:26
  297.0 1.4 collective-permute-done.29
  298.5 2.4 collective-permute-start.31
  302.5 2.0 collective-permute-done.32
  305.3 63.6 %all-reduce = (f32[]{:T(128)}, f32[]{:T(128)}) all-reduce(f32[]{:T(128)} %get-tuple-element.4, f32[]{:T(128)} %get-tuple-element.3), channel_id=1, replica_groups=mesh['gx'=16,'gy'=2] {'gx','gy'}, use_global_device_ids=true, to_apply=%region_21.22 | all-reduce | flops 2 | bytes 16 | tf_op jit(solution)/shard_map/psum | solution.py:63
  374.0 4.4 %collective-permute-start.34 = (f32[128,1]{1,0:T(8,128)S(1)}, f32[128,1]{1,0:T(8,128)S(1)}, u32[]{:S(2)}, u32[]{:S(2)}) collective-permute-start(f32[128,1]{1,0:T(8,128)S(1)} %get-tuple-element.70), channel_id=1, source_target_pairs={{2,0},{4,2},{6,4},{8,6},{10,8},{12,10},{14,12},{16,14},{18,16},{20... | collective-permute-start | bytes 1544 | tf_op jit(solution)/shard_map/ppermute | solution.py:26
  378.4 2.0 collective-permute-done.33
  380.5 2.4 collective-permute-start.35
  383.6 1.2 copy.18
  386.0 2.0 collective-permute-start.2
  389.9 1.9 collective-permute-done.3
  391.8 2.3 maximum_select_fusion
  395.4 3.3 bitcast_multiply_fusion
  (117 shorter events, 19.5 us)
Async XLA Ops:
  0.6 10.6 %copy-start.11 = (f32[128,128]{1,0:T(8,128)S(1)}, f32[128,128]{1,0:T(8,128)}, u32[]{:S(2)}) copy-start(f32[128,128]{1,0:T(8,128)} %param.17) | copy-start | bytes 196612
  0.6 7.9 %copy-start.14 = (f32[128,128]{1,0:T(8,128)S(1)}, f32[128,128]{1,0:T(8,128)}, u32[]{:S(2)}) copy-start(f32[128,128]{1,0:T(8,128)} %param.10) | copy-start | bytes 196612
  1.8 20.0 %copy-start.12 = (f32[8,128,128]{2,1,0:T(8,128)}, f32[8,128,128]{2,1,0:T(8,128)S(1)}, u32[]{:S(2)}) copy-start(f32[8,128,128]{2,1,0:T(8,128)S(1)} %convert_element_type.3) | copy-start | bytes 1572868
  2.9 8.3 %collective-permute-start.5 = (f32[2,128,1]{2,1,0:T(8,128)S(1)}, f32[2,128,1]{2,1,0:T(8,128)S(1)}, u32[]{:S(2)}, u32[]{:S(2)}) collective-permute-start(f32[2,128,1]{2,1,0:T(8,128)S(1)} %get-tuple-element.67), channel_id=1, source_target_pairs={{0,2},{2,4},{4,6},{6,8},{8,10},{10,12},{12,14},{14,16},{16,18},{18... | collective-permute-start | bytes 3080 | tf_op jit(solution)/shard_map/ppermute | solution.py:23
  3.5 7.7 %collective-permute-start.6 = (f32[2,128,1]{2,1,0:T(8,128)S(1)}, f32[2,128,1]{2,1,0:T(8,128)S(1)}, u32[]{:S(2)}, u32[]{:S(2)}) collective-permute-start(f32[2,128,1]{2,1,0:T(8,128)S(1)} %get-tuple-element.68), channel_id=1, source_target_pairs={{2,0},{4,2},{6,4},{8,6},{10,8},{12,10},{14,12},{16,14},{18,16},{20... | collective-permute-start | bytes 3080 | tf_op jit(solution)/shard_map/ppermute | solution.py:26
  8.6 4.8 %collective-permute-start.10 = (f32[128,1]{1,0:T(8,128)S(1)}, f32[128,1]{1,0:T(8,128)S(1)}, u32[]{:S(2)}, u32[]{:S(2)}) collective-permute-start(f32[128,1]{1,0:T(8,128)S(1)} %get-tuple-element.82), channel_id=1, source_target_pairs={{2,0},{4,2},{6,4},{8,6},{10,8},{12,10},{14,12},{16,14},{18,16},{20... | collective-permute-start | bytes 1544 | tf_op jit(solution)/shard_map/ppermute | solution.py:26
  9.3 6.4 %collective-permute-start.9 = (f32[128,1]{1,0:T(8,128)S(1)}, f32[128,1]{1,0:T(8,128)S(1)}, u32[]{:S(2)}, u32[]{:S(2)}) collective-permute-start(f32[128,1]{1,0:T(8,128)S(1)} %get-tuple-element.81), channel_id=1, source_target_pairs={{0,2},{2,4},{4,6},{6,8},{8,10},{10,12},{12,14},{14,16},{16,18},{18... | collective-permute-start | bytes 1544 | tf_op jit(solution)/shard_map/ppermute | solution.py:23
  11.3 6.5 %collective-permute-start.7 = (f32[2,1,130]{2,1,0:T(1,128)S(1)}, f32[2,1,130]{2,1,0:T(1,128)S(1)}, u32[]{:S(2)}, u32[]{:S(2)}) collective-permute-start(f32[2,1,130]{2,1,0:T(1,128)S(1)} %get-tuple-element.49), channel_id=1, source_target_pairs={{0,1},{1,0},{2,3},{3,2},{4,5},{5,4},{6,7},{7,6},{8,9},{9,8},{10,11... | collective-permute-start | bytes 3128 | tf_op jit(solution)/shard_map/ppermute | solution.py:23
  13.3 4.5 %collective-permute-start.8 = (f32[2,1,130]{2,1,0:T(1,128)S(1)}, f32[2,1,130]{2,1,0:T(1,128)S(1)}, u32[]{:S(2)}, u32[]{:S(2)}) collective-permute-start(f32[2,1,130]{2,1,0:T(1,128)S(1)} %get-tuple-element.50), channel_id=1, source_target_pairs={{1,0},{0,1},{3,2},{2,3},{5,4},{4,5},{7,6},{6,7},{9,8},{8,9},{11,10... | collective-permute-start | bytes 3128 | tf_op jit(solution)/shard_map/ppermute | solution.py:26
  15.8 3.6 collective-permute-start.11
  17.3 3.6 collective-permute-start.12
  18.0 103.8 %copy-start.7 = (s32[8,128,128]{2,1,0:T(8,128)S(1)}, s32[8,128,128]{2,1,0:T(8,128)}, u32[]{:S(2)}) copy-start(s32[8,128,128]{2,1,0:T(8,128)} %param.16) | copy-start | bytes 1572868
  18.0 103.8 %copy-start.9 = (f32[8,128,128]{2,1,0:T(8,128)S(1)}, f32[8,128,128]{2,1,0:T(8,128)}, u32[]{:S(2)}) copy-start(f32[8,128,128]{2,1,0:T(8,128)} %param.9) | copy-start | bytes 1572868
  60.3 66.3 %copy-start = (f32[8,128,128]{2,1,0:T(8,128)S(1)}, f32[8,128,128]{2,1,0:T(8,128)}, u32[]{:S(2)}) copy-start(f32[8,128,128]{2,1,0:T(8,128)} %param.12) | copy-start | bytes 1572868
  60.3 66.3 %copy-start.2 = (f32[8,128,128]{2,1,0:T(8,128)S(1)}, f32[8,128,128]{2,1,0:T(8,128)}, u32[]{:S(2)}) copy-start(f32[8,128,128]{2,1,0:T(8,128)} %param.11) | copy-start | bytes 1572868
  60.3 6.5 %collective-permute-start.13 = (f32[128,1]{1,0:T(8,128)S(1)}, f32[128,1]{1,0:T(8,128)S(1)}, u32[]{:S(2)}, u32[]{:S(2)}) collective-permute-start(f32[128,1]{1,0:T(8,128)S(1)} %get-tuple-element.79), channel_id=1, source_target_pairs={{0,2},{2,4},{4,6},{6,8},{8,10},{10,12},{12,14},{14,16},{16,18},{18... | collective-permute-start | bytes 1544 | tf_op jit(solution)/shard_map/ppermute | solution.py:23
  60.3 6.5 %collective-permute-start.14 = (f32[128,1]{1,0:T(8,128)S(1)}, f32[128,1]{1,0:T(8,128)S(1)}, u32[]{:S(2)}, u32[]{:S(2)}) collective-permute-start(f32[128,1]{1,0:T(8,128)S(1)} %get-tuple-element.80), channel_id=1, source_target_pairs={{2,0},{4,2},{6,4},{8,6},{10,8},{12,10},{14,12},{16,14},{18,16},{20... | collective-permute-start | bytes 1544 | tf_op jit(solution)/shard_map/ppermute | solution.py:26
  66.9 3.9 collective-permute-start.15
  69.3 3.6 collective-permute-start.16
  117.4 6.5 %collective-permute-start.17 = (f32[128,1]{1,0:T(8,128)S(1)}, f32[128,1]{1,0:T(8,128)S(1)}, u32[]{:S(2)}, u32[]{:S(2)}) collective-permute-start(f32[128,1]{1,0:T(8,128)S(1)} %get-tuple-element.77), channel_id=1, source_target_pairs={{0,2},{2,4},{4,6},{6,8},{8,10},{10,12},{12,14},{14,16},{16,18},{18... | collective-permute-start | bytes 1544 | tf_op jit(solution)/shard_map/ppermute | solution.py:23
  117.5 6.5 %collective-permute-start.18 = (f32[128,1]{1,0:T(8,128)S(1)}, f32[128,1]{1,0:T(8,128)S(1)}, u32[]{:S(2)}, u32[]{:S(2)}) collective-permute-start(f32[128,1]{1,0:T(8,128)S(1)} %get-tuple-element.78), channel_id=1, source_target_pairs={{2,0},{4,2},{6,4},{8,6},{10,8},{12,10},{14,12},{16,14},{18,16},{20... | collective-permute-start | bytes 1544 | tf_op jit(solution)/shard_map/ppermute | solution.py:26
  124.0 4.0 %collective-permute-start.19 = (f32[1,130]{1,0:T(1,128)S(1)}, f32[1,130]{1,0:T(1,128)S(1)}, u32[]{:S(2)}, u32[]{:S(2)}) collective-permute-start(f32[1,130]{1,0:T(1,128)S(1)} %get-tuple-element.61), channel_id=1, source_target_pairs={{0,1},{1,0},{2,3},{3,2},{4,5},{5,4},{6,7},{7,6},{8,9},{9,8},{10,11... | collective-permute-start | bytes 1568 | tf_op jit(solution)/shard_map/ppermute | solution.py:23
  126.4 3.6 collective-permute-start.20
  172.7 13.6 %collective-permute-start.21 = (f32[128,1]{1,0:T(8,128)}, f32[128,1]{1,0:T(8,128)S(1)}, u32[]{:S(2)}, u32[]{:S(2)}) collective-permute-start(f32[128,1]{1,0:T(8,128)} %get-tuple-element.75), channel_id=1, source_target_pairs={{0,2},{2,4},{4,6},{6,8},{8,10},{10,12},{12,14},{14,16},{16,18},{18... | collective-permute-start | bytes 1544 | tf_op jit(solution)/shard_map/ppermute | solution.py:23
  172.7 13.6 %collective-permute-start.22 = (f32[128,1]{1,0:T(8,128)}, f32[128,1]{1,0:T(8,128)S(1)}, u32[]{:S(2)}, u32[]{:S(2)}) collective-permute-start(f32[128,1]{1,0:T(8,128)} %get-tuple-element.76), channel_id=1, source_target_pairs={{2,0},{4,2},{6,4},{8,6},{10,8},{12,10},{14,12},{16,14},{18,16},{20... | collective-permute-start | bytes 1544 | tf_op jit(solution)/shard_map/ppermute | solution.py:26
  179.3 9.6 %copy-start.15 = (s32[1,1,8]{2,1,0:T(1,128)S(1)}, s32[1,1,8]{2,1,0:T(1,128)}, u32[]{:S(2)}) copy-start(s32[1,1,8]{2,1,0:T(1,128)} %param.15) | copy-start | bytes 100
  181.3 201.8 %collective-permute-start = (f32[3,8,128,1]{2,1,3,0:T(8,128)S(1)}, f32[3,8,128,1]{2,1,3,0:T(8,128)S(1)}, u32[]{:S(2)}, u32[]{:S(2)}) collective-permute-start(f32[3,8,128,1]{2,1,3,0:T(8,128)S(1)} %copy.15), channel_id=1, source_target_pairs={{0,2},{2,4},{4,6},{6,8},{8,10},{10,12},{12,14},{14,16},{16,18},{18... | collective-permute-start | bytes 36872 | tf_op jit(solution)/shard_map/ppermute | solution.py:23
  181.8 201.8 %collective-permute-start.1 = (f32[3,8,128,1]{2,1,3,0:T(8,128)S(1)}, f32[3,8,128,1]{2,1,3,0:T(8,128)}, u32[]{:S(2)}, u32[]{:S(2)}) collective-permute-start(f32[3,8,128,1]{2,1,3,0:T(8,128)S(1)} %copy.16), channel_id=1, source_target_pairs={{2,0},{4,2},{6,4},{8,6},{10,8},{12,10},{14,12},{16,14},{18,16},{20... | collective-permute-start | bytes 36872 | tf_op jit(solution)/shard_map/ppermute | solution.py:26
  186.3 4.0 %collective-permute-start.23 = (f32[1,130]{1,0:T(1,128)S(1)}, f32[1,130]{1,0:T(1,128)S(1)}, u32[]{:S(2)}, u32[]{:S(2)}) collective-permute-start(f32[1,130]{1,0:T(1,128)S(1)} %get-tuple-element.59), channel_id=1, source_target_pairs={{0,1},{1,0},{2,3},{3,2},{4,5},{5,4},{6,7},{7,6},{8,9},{9,8},{10,11... | collective-permute-start | bytes 1568 | tf_op jit(solution)/shard_map/ppermute | solution.py:23
  188.8 3.6 collective-permute-start.24
  235.1 6.5 %collective-permute-start.25 = (f32[128,1]{1,0:T(8,128)S(1)}, f32[128,1]{1,0:T(8,128)S(1)}, u32[]{:S(2)}, u32[]{:S(2)}) collective-permute-start(f32[128,1]{1,0:T(8,128)S(1)} %get-tuple-element.73), channel_id=1, source_target_pairs={{0,2},{2,4},{4,6},{6,8},{8,10},{10,12},{12,14},{14,16},{16,18},{18... | collective-permute-start | bytes 1544 | tf_op jit(solution)/shard_map/ppermute | solution.py:23
  235.2 6.5 %collective-permute-start.26 = (f32[128,1]{1,0:T(8,128)S(1)}, f32[128,1]{1,0:T(8,128)S(1)}, u32[]{:S(2)}, u32[]{:S(2)}) collective-permute-start(f32[128,1]{1,0:T(8,128)S(1)} %get-tuple-element.74), channel_id=1, source_target_pairs={{2,0},{4,2},{6,4},{8,6},{10,8},{12,10},{14,12},{16,14},{18,16},{20... | collective-permute-start | bytes 1544 | tf_op jit(solution)/shard_map/ppermute | solution.py:26
  241.7 4.0 %collective-permute-start.27 = (f32[1,130]{1,0:T(1,128)S(1)}, f32[1,130]{1,0:T(1,128)S(1)}, u32[]{:S(2)}, u32[]{:S(2)}) collective-permute-start(f32[1,130]{1,0:T(1,128)S(1)} %get-tuple-element.57), channel_id=1, source_target_pairs={{0,1},{1,0},{2,3},{3,2},{4,5},{5,4},{6,7},{7,6},{8,9},{9,8},{10,11... | collective-permute-start | bytes 1568 | tf_op jit(solution)/shard_map/ppermute | solution.py:23
  244.2 3.6 collective-permute-start.28
  291.9 6.5 %collective-permute-start.29 = (f32[128,1]{1,0:T(8,128)S(1)}, f32[128,1]{1,0:T(8,128)S(1)}, u32[]{:S(2)}, u32[]{:S(2)}) collective-permute-start(f32[128,1]{1,0:T(8,128)S(1)} %get-tuple-element.71), channel_id=1, source_target_pairs={{0,2},{2,4},{4,6},{6,8},{8,10},{10,12},{12,14},{14,16},{16,18},{18... | collective-permute-start | bytes 1544 | tf_op jit(solution)/shard_map/ppermute | solution.py:23
  291.9 6.5 %collective-permute-start.30 = (f32[128,1]{1,0:T(8,128)S(1)}, f32[128,1]{1,0:T(8,128)S(1)}, u32[]{:S(2)}, u32[]{:S(2)}) collective-permute-start(f32[128,1]{1,0:T(8,128)S(1)} %get-tuple-element.72), channel_id=1, source_target_pairs={{2,0},{4,2},{6,4},{8,6},{10,8},{12,10},{14,12},{16,14},{18,16},{20... | collective-permute-start | bytes 1544 | tf_op jit(solution)/shard_map/ppermute | solution.py:26
  298.5 4.0 %collective-permute-start.31 = (f32[1,130]{1,0:T(1,128)S(1)}, f32[1,130]{1,0:T(1,128)S(1)}, u32[]{:S(2)}, u32[]{:S(2)}) collective-permute-start(f32[1,130]{1,0:T(1,128)S(1)} %get-tuple-element.55), channel_id=1, source_target_pairs={{0,1},{1,0},{2,3},{3,2},{4,5},{5,4},{6,7},{7,6},{8,9},{9,8},{10,11... | collective-permute-start | bytes 1568 | tf_op jit(solution)/shard_map/ppermute | solution.py:23
  300.9 3.6 collective-permute-start.32
  302.2 92.3 %collective-permute-start.4 = (f32[2,8,128,128]{3,2,0,1:T(8,128)}, f32[2,8,128,128]{3,2,0,1:T(8,128)}, u32[]{:S(2)}, u32[]{:S(2)}) collective-permute-start(f32[2,8,128,128]{3,2,0,1:T(8,128)} %select_bitcast_fusion), channel_id=1, source_target_pairs={{0,16},{2,18},{4,20},{6,22},{8,24},{10,26},{12,28},{14,30},{16,0},... | collective-permute-start | bytes 3145736 | tf_op jit(solution)/shard_map/ppermute | solution.py:34
  373.9 6.5 %collective-permute-start.33 = (f32[128,1]{1,0:T(8,128)S(1)}, f32[128,1]{1,0:T(8,128)S(1)}, u32[]{:S(2)}, u32[]{:S(2)}) collective-permute-start(f32[128,1]{1,0:T(8,128)S(1)} %get-tuple-element.69), channel_id=1, source_target_pairs={{0,2},{2,4},{4,6},{6,8},{8,10},{10,12},{12,14},{14,16},{16,18},{18... | collective-permute-start | bytes 1544 | tf_op jit(solution)/shard_map/ppermute | solution.py:23
  374.0 6.5 %collective-permute-start.34 = (f32[128,1]{1,0:T(8,128)S(1)}, f32[128,1]{1,0:T(8,128)S(1)}, u32[]{:S(2)}, u32[]{:S(2)}) collective-permute-start(f32[128,1]{1,0:T(8,128)S(1)} %get-tuple-element.70), channel_id=1, source_target_pairs={{2,0},{4,2},{6,4},{8,6},{10,8},{12,10},{14,12},{16,14},{18,16},{20... | collective-permute-start | bytes 1544 | tf_op jit(solution)/shard_map/ppermute | solution.py:26
  380.5 7.6 %collective-permute-start.35 = (f32[1,130]{1,0:T(1,128)S(1)}, f32[1,130]{1,0:T(1,128)S(1)}, u32[]{:S(2)}, u32[]{:S(2)}) collective-permute-start(f32[1,130]{1,0:T(1,128)S(1)} %get-tuple-element.53), channel_id=1, source_target_pairs={{0,1},{1,0},{2,3},{3,2},{4,5},{5,4},{6,7},{7,6},{8,9},{9,8},{10,11... | collective-permute-start | bytes 1568 | tf_op jit(solution)/shard_map/ppermute | solution.py:23
  383.0 5.1 %collective-permute-start.36 = (f32[1,130]{1,0:T(1,128)S(1)}, f32[1,130]{1,0:T(1,128)S(1)}, u32[]{:S(2)}, u32[]{:S(2)}) collective-permute-start(f32[1,130]{1,0:T(1,128)S(1)} %get-tuple-element.54), channel_id=1, source_target_pairs={{1,0},{0,1},{3,2},{2,3},{5,4},{4,5},{7,6},{6,7},{9,8},{8,9},{11,10... | collective-permute-start | bytes 1568 | tf_op jit(solution)/shard_map/ppermute | solution.py:26
  384.8 7.1 %copy-start.1 = (f32[8,128,128]{2,1,0:T(8,128)S(1)}, f32[8,128,128]{2,1,0:T(8,128)}, u32[]{:S(2)}) copy-start(f32[8,128,128]{2,1,0:T(8,128)} %param.12) | copy-start | bytes 1572868
  384.8 7.0 %copy-start.3 = (f32[8,128,128]{2,1,0:T(8,128)S(1)}, f32[8,128,128]{2,1,0:T(8,128)}, u32[]{:S(2)}) copy-start(f32[8,128,128]{2,1,0:T(8,128)} %param.11) | copy-start | bytes 1572868
  384.8 7.0 %copy-start.5 = (f32[1,8,128,128]{3,2,1,0:T(8,128)S(1)}, f32[1,8,128,128]{3,2,1,0:T(8,128)}, u32[]{:S(2)}) copy-start(f32[1,8,128,128]{3,2,1,0:T(8,128)} %copy-done.4) | copy-start | bytes 1572868
  386.0 3.9 collective-permute-start.2
  388.0 3.8 collective-permute-start.3
  (5 other events, 13.1 us)
where the time goes:
time: 400 us; the launch traced here: 399 us
  blocking collectives  253 us (63%)
  starting transfers between devices  58.8 us (15%)
  waiting for transfers between devices  34 us (8%)
  between operations  22.8 us (6%)
  other arithmetic  20.2 us (5%)
  local copies, waits for them, and re-layouts  9.43 us (2%)
    psum x6, blocking collectives, paired(): lax.psum((jnp.sum(residual * residual), jnp.sum(residual * image_field)),...  253 us
    ppermute x18, starting transfers between devices, padded_2(): lax.ppermute(lax.slice_in_dim(block, 0, width, axis=dim), axis, backward)  37.9 us
    ppermute x18, starting transfers between devices, padded_2(): lax.ppermute(lax.slice_in_dim(block, block.shape[dim] - width, None, axis...  21 us
    ppermute x18, waiting for transfers between devices, padded_2(): lax.ppermute(lax.slice_in_dim(block, block.shape[dim] - width, None, axis...  20.4 us
    ppermute x18, waiting for transfers between devices, padded_2(): lax.ppermute(lax.slice_in_dim(block, 0, width, axis=dim), axis, backward)  13.6 us
  transfers between devices with their start and end apart: 37, of which 21 were waited for; matrix products, arithmetic and copies ran while one was open for 5% of the time, Pallas kernels for 0%

commit v1 on v0

--- a/solution.py
+++ b/solution.py
@@ -60,7 +60,9 @@
 
 
 def paired(residual, image_field):
-    return lax.psum((jnp.sum(residual * residual), jnp.sum(residual * image_field)), ("gx", "gy"))
+    return lax.psum(
+        lax.psum((jnp.sum(residual * residual), jnp.sum(residual * image_field)), "gy"), "gx"
+    )
 
 
 def body(

time: 400 us -> 374 us (0.935); the launches traced: 399 us -> 367 us
  blocking collectives: 253 us -> 231 us
  waiting for transfers between devices: 34 us -> 27.9 us
    psum x6, blocking collectives: 253 us -> 33.6 us  [paired(): lax.psum((jnp.sum(residual * residual), jnp.sum(residual * image_field)),...]
    psum x0 -> x6, blocking collectives: none -> 197 us  [paired(): lax.psum(lax.psum((jnp.sum(residual * residual), jnp.sum(residual * image...]
    ppermute x18, starting transfers between devices: 21 us -> 13.5 us  [padded_2(): lax.ppermute(lax.slice_in_dim(block, block.shape[dim] - width, None, axis...]
    ppermute x18, waiting for transfers between devices: 13.6 us -> 7.54 us  [padded_2(): lax.ppermute(lax.slice_in_dim(block, 0, width, axis=dim), axis, backward)]
    ppermute x18, starting transfers between devices: 37.9 us -> 42.9 us  [padded_2(): lax.ppermute(lax.slice_in_dim(block, 0, width, axis=dim), axis, backward)]
  transfers between devices with their start and end apart: 37 -> 37, of which waited for: 21 -> 22; matrix products, arithmetic and copies ran while one was open for 5% -> 5% of each run, Pallas kernels for 0% -> 0%
where the time goes in v1:
time: 374 us; the launch traced here: 367 us
  blocking collectives  231 us (62%)
  starting transfers between devices  56.4 us (15%)
  waiting for transfers between devices  27.9 us (7%)
  between operations  22.6 us (6%)
  other arithmetic  20.2 us (5%)
  local copies, waits for them, and re-layouts  9.44 us (3%)
    psum x6, blocking collectives, paired(): lax.psum(lax.psum((jnp.sum(residual * residual), jnp.sum(residual * image...  197 us
    ppermute x18, starting transfers between devices, padded_2(): lax.ppermute(lax.slice_in_dim(block, 0, width, axis=dim), axis, backward)  42.9 us
    psum x6, blocking collectives, paired(): lax.psum((jnp.sum(residual * residual), jnp.sum(residual * image_field)),...  33.6 us
    ppermute x18, waiting for transfers between devices, padded_2(): lax.ppermute(lax.slice_in_dim(block, block.shape[dim] - width, None, axis...  20.3 us
    ppermute x18, starting transfers between devices, padded_2(): lax.ppermute(lax.slice_in_dim(block, block.shape[dim] - width, None, axis...  13.5 us
    ppermute x18, waiting for transfers between devices, padded_2(): lax.ppermute(lax.slice_in_dim(block, 0, width, axis=dim), axis, backward)  7.54 us
  transfers between devices with their start and end apart: 37, of which 22 were waited for; matrix products, arithmetic and copies ran while one was open for 5% of the time, Pallas kernels for 0%

profile of v1, /device:TPU:0, one launch (start us, length us, event | category | flops | bytes accessed | tf_op | source)
XLA Modules:
  0.0 367.1 jit_solution(5566582060140123170)
XLA Ops:
  3.5 5.0 %collective-permute-start.6 = (f32[2,128,1]{2,1,0:T(8,128)S(1)}, f32[2,128,1]{2,1,0:T(8,128)S(1)}, u32[]{:S(2)}, u32[]{:S(2)}) collective-permute-start(f32[2,128,1]{2,1,0:T(8,128)S(1)} %get-tuple-element.80), channel_id=1, source_target_pairs={{2,0},{4,2},{6,4},{8,6},{10,8},{12,10},{14,12},{16,14},{18,16},{20... | collective-permute-start | bytes 3080 | tf_op jit(solution)/shard_map/ppermute | solution.py:26
  9.3 1.9 collective-permute-done.5
  11.3 2.1 collective-permute-start.7
  13.4 2.3 collective-permute-done.9
  15.8 1.5 collective-permute-start.11
  19.3 1.5 collective-permute-done.12
  21.7 5.5 %all-reduce.11 = (f32[]{:T(128)}, f32[]{:T(128)}) all-reduce(f32[]{:T(128)} %get-tuple-element.14, f32[]{:T(128)} %get-tuple-element.13), channel_id=1, replica_groups=mesh['gx'=16,'gy'=2] {'gy'}, use_global_device_ids=true, to_apply=%region_1.2 | all-reduce | flops 2 | bytes 16 | tf_op jit(solution)/shard_map/psum | solution.py:64
  27.3 30.1 %all-reduce.5 = (f32[]{:T(128)}, f32[]{:T(128)}) all-reduce(f32[]{:T(128)} %get-tuple-element.37, f32[]{:T(128)} %get-tuple-element.38), channel_id=1, replica_groups=mesh['gx'=16,'gy'=2] {'gx'}, use_global_device_ids=true, to_apply=%region_2.3 | all-reduce | flops 2 | bytes 16 | tf_op jit(solution)/shard_map/psum | solution.py:63
  58.9 4.4 %collective-permute-start.14 = (f32[128,1]{1,0:T(8,128)S(1)}, f32[128,1]{1,0:T(8,128)S(1)}, u32[]{:S(2)}, u32[]{:S(2)}) collective-permute-start(f32[128,1]{1,0:T(8,128)S(1)} %get-tuple-element.92), channel_id=1, source_target_pairs={{2,0},{4,2},{6,4},{8,6},{10,8},{12,10},{14,12},{16,14},{18,16},{20... | collective-permute-start | bytes 1544 | tf_op jit(solution)/shard_map/ppermute | solution.py:26
  63.3 1.9 collective-permute-done.13
  65.9 1.5 collective-permute-start.16
  67.4 1.5 collective-permute-done.15
  70.3 5.6 %all-reduce.10 = (f32[]{:T(128)}, f32[]{:T(128)}) all-reduce(f32[]{:T(128)} %get-tuple-element.12, f32[]{:T(128)} %get-tuple-element.11), channel_id=1, replica_groups=mesh['gx'=16,'gy'=2] {'gy'}, use_global_device_ids=true, to_apply=%region_7.8 | all-reduce | flops 2 | bytes 16 | tf_op jit(solution)/shard_map/psum | solution.py:64
  75.9 32.0 %all-reduce.4 = (f32[]{:T(128)}, f32[]{:T(128)}) all-reduce(f32[]{:T(128)} %get-tuple-element.35, f32[]{:T(128)} %get-tuple-element.36), channel_id=1, replica_groups=mesh['gx'=16,'gy'=2] {'gx'}, use_global_device_ids=true, to_apply=%region_8.9 | all-reduce | flops 2 | bytes 16 | tf_op jit(solution)/shard_map/psum | solution.py:63
  112.7 4.4 %collective-permute-start.18 = (f32[128,1]{1,0:T(8,128)S(1)}, f32[128,1]{1,0:T(8,128)S(1)}, u32[]{:S(2)}, u32[]{:S(2)}) collective-permute-start(f32[128,1]{1,0:T(8,128)S(1)} %get-tuple-element.90), channel_id=1, source_target_pairs={{2,0},{4,2},{6,4},{8,6},{10,8},{12,10},{14,12},{16,14},{18,16},{20... | collective-permute-start | bytes 1544 | tf_op jit(solution)/shard_map/ppermute | solution.py:26
  117.2 1.9 collective-permute-done.17
  119.2 1.5 collective-permute-start.19
  121.4 1.4 collective-permute-done.19
  122.7 1.5 collective-permute-done.20
  125.0 5.6 %all-reduce.9 = (f32[]{:T(128)}, f32[]{:T(128)}) all-reduce(f32[]{:T(128)} %get-tuple-element.10, f32[]{:T(128)} %get-tuple-element.9), channel_id=1, replica_groups=mesh['gx'=16,'gy'=2] {'gy'}, use_global_device_ids=true, to_apply=%region_13.14 | all-reduce | flops 2 | bytes 16 | tf_op jit(solution)/shard_map/psum | solution.py:64
  130.6 32.0 %all-reduce.3 = (f32[]{:T(128)}, f32[]{:T(128)}) all-reduce(f32[]{:T(128)} %get-tuple-element.33, f32[]{:T(128)} %get-tuple-element.34), channel_id=1, replica_groups=mesh['gx'=16,'gy'=2] {'gx'}, use_global_device_ids=true, to_apply=%region_14.15 | all-reduce | flops 2 | bytes 16 | tf_op jit(solution)/shard_map/psum | solution.py:63
  167.2 4.4 %collective-permute-start.22 = (f32[128,1]{1,0:T(8,128)}, f32[128,1]{1,0:T(8,128)S(1)}, u32[]{:S(2)}, u32[]{:S(2)}) collective-permute-start(f32[128,1]{1,0:T(8,128)} %get-tuple-element.88), channel_id=1, source_target_pairs={{2,0},{4,2},{6,4},{8,6},{10,8},{12,10},{14,12},{16,14},{18,16},{20... | collective-permute-start | bytes 1544 | tf_op jit(solution)/shard_map/ppermute | solution.py:26
  171.7 2.2 fusion.119
  173.9 2.0 copy.15
  176.4 4.4 %collective-permute-start.1 = (f32[3,8,128,1]{2,1,3,0:T(8,128)S(1)}, f32[3,8,128,1]{2,1,3,0:T(8,128)}, u32[]{:S(2)}, u32[]{:S(2)}) collective-permute-start(f32[3,8,128,1]{2,1,3,0:T(8,128)S(1)} %copy.16), channel_id=1, source_target_pairs={{2,0},{4,2},{6,4},{8,6},{10,8},{12,10},{14,12},{16,14},{18,16},{20... | collective-permute-start | bytes 36872 | tf_op jit(solution)/shard_map/ppermute | solution.py:26
  181.4 1.5 collective-permute-start.24
  183.0 1.5 collective-permute-done.23
  185.0 1.7 multiply_reduce_fusion.3
  186.7 5.6 %all-reduce.8 = (f32[]{:T(128)}, f32[]{:T(128)}) all-reduce(f32[]{:T(128)} %get-tuple-element.8, f32[]{:T(128)} %get-tuple-element.7), channel_id=1, replica_groups=mesh['gx'=16,'gy'=2] {'gy'}, use_global_device_ids=true, to_apply=%region_19.20 | all-reduce | flops 2 | bytes 16 | tf_op jit(solution)/shard_map/psum | solution.py:64
  192.3 30.2 %all-reduce.2 = (f32[]{:T(128)}, f32[]{:T(128)}) all-reduce(f32[]{:T(128)} %get-tuple-element.31, f32[]{:T(128)} %get-tuple-element.32), channel_id=1, replica_groups=mesh['gx'=16,'gy'=2] {'gx'}, use_global_device_ids=true, to_apply=%region_20.21 | all-reduce | flops 2 | bytes 16 | tf_op jit(solution)/shard_map/psum | solution.py:63
  226.6 4.4 %collective-permute-start.26 = (f32[128,1]{1,0:T(8,128)S(1)}, f32[128,1]{1,0:T(8,128)S(1)}, u32[]{:S(2)}, u32[]{:S(2)}) collective-permute-start(f32[128,1]{1,0:T(8,128)S(1)} %get-tuple-element.86), channel_id=1, source_target_pairs={{2,0},{4,2},{6,4},{8,6},{10,8},{12,10},{14,12},{16,14},{18,16},{20... | collective-permute-start | bytes 1544 | tf_op jit(solution)/shard_map/ppermute | solution.py:26
  231.0 1.9 collective-permute-done.25
  233.0 1.5 collective-permute-start.27
  236.6 1.5 collective-permute-done.28
  239.0 5.6 %all-reduce.7 = (f32[]{:T(128)}, f32[]{:T(128)}) all-reduce(f32[]{:T(128)} %get-tuple-element.6, f32[]{:T(128)} %get-tuple-element.5), channel_id=1, replica_groups=mesh['gx'=16,'gy'=2] {'gy'}, use_global_device_ids=true, to_apply=%region_25.26 | all-reduce | flops 2 | bytes 16 | tf_op jit(solution)/shard_map/psum | solution.py:64
  244.6 32.0 %all-reduce.1 = (f32[]{:T(128)}, f32[]{:T(128)}) all-reduce(f32[]{:T(128)} %get-tuple-element.29, f32[]{:T(128)} %get-tuple-element.30), channel_id=1, replica_groups=mesh['gx'=16,'gy'=2] {'gx'}, use_global_device_ids=true, to_apply=%region_26.27 | all-reduce | flops 2 | bytes 16 | tf_op jit(solution)/shard_map/psum | solution.py:63
  280.6 4.4 %collective-permute-start.30 = (f32[128,1]{1,0:T(8,128)S(1)}, f32[128,1]{1,0:T(8,128)S(1)}, u32[]{:S(2)}, u32[]{:S(2)}) collective-permute-start(f32[128,1]{1,0:T(8,128)S(1)} %get-tuple-element.84), channel_id=1, source_target_pairs={{2,0},{4,2},{6,4},{8,6},{10,8},{12,10},{14,12},{16,14},{18,16},{20... | collective-permute-start | bytes 1544 | tf_op jit(solution)/shard_map/ppermute | solution.py:26
  285.7 1.4 collective-permute-done.29
  288.3 1.4 collective-permute-start.32
  292.7 5.6 %all-reduce.6 = (f32[]{:T(128)}, f32[]{:T(128)}) all-reduce(f32[]{:T(128)} %get-tuple-element.4, f32[]{:T(128)} %get-tuple-element.3), channel_id=1, replica_groups=mesh['gx'=16,'gy'=2] {'gy'}, use_global_device_ids=true, to_apply=%region_31.32 | all-reduce | flops 2 | bytes 16 | tf_op jit(solution)/shard_map/psum | solution.py:64
  298.3 40.7 %all-reduce = (f32[]{:T(128)}, f32[]{:T(128)}) all-reduce(f32[]{:T(128)} %get-tuple-element.27, f32[]{:T(128)} %get-tuple-element.28), channel_id=1, replica_groups=mesh['gx'=16,'gy'=2] {'gx'}, use_global_device_ids=true, to_apply=%region_32.33 | all-reduce | flops 2 | bytes 16 | tf_op jit(solution)/shard_map/psum | solution.py:63
  343.6 3.1 collective-permute-start.33
  346.7 1.8 collective-permute-start.34
  348.6 1.9 collective-permute-done.33
  351.2 1.4 collective-permute-start.36
  356.2 1.4 collective-permute-start.3
  360.2 2.3 maximum_select_fusion
  363.7 3.3 bitcast_multiply_fusion
  (123 shorter events, 29.8 us)
Async XLA Ops:
  0.6 10.6 %copy-start.11 = (f32[128,128]{1,0:T(8,128)S(1)}, f32[128,128]{1,0:T(8,128)}, u32[]{:S(2)}) copy-start(f32[128,128]{1,0:T(8,128)} %param.17) | copy-start | bytes 196612
  0.6 7.9 %copy-start.14 = (f32[128,128]{1,0:T(8,128)S(1)}, f32[128,128]{1,0:T(8,128)}, u32[]{:S(2)}) copy-start(f32[128,128]{1,0:T(8,128)} %param.10) | copy-start | bytes 196612
  1.8 20.0 %copy-start.12 = (f32[8,128,128]{2,1,0:T(8,128)}, f32[8,128,128]{2,1,0:T(8,128)S(1)}, u32[]{:S(2)}) copy-start(f32[8,128,128]{2,1,0:T(8,128)S(1)} %convert_element_type.3) | copy-start | bytes 1572868
  2.9 8.3 %collective-permute-start.5 = (f32[2,128,1]{2,1,0:T(8,128)S(1)}, f32[2,128,1]{2,1,0:T(8,128)S(1)}, u32[]{:S(2)}, u32[]{:S(2)}) collective-permute-start(f32[2,128,1]{2,1,0:T(8,128)S(1)} %get-tuple-element.79), channel_id=1, source_target_pairs={{0,2},{2,4},{4,6},{6,8},{8,10},{10,12},{12,14},{14,16},{16,18},{18... | collective-permute-start | bytes 3080 | tf_op jit(solution)/shard_map/ppermute | solution.py:23
  3.5 7.7 %collective-permute-start.6 = (f32[2,128,1]{2,1,0:T(8,128)S(1)}, f32[2,128,1]{2,1,0:T(8,128)S(1)}, u32[]{:S(2)}, u32[]{:S(2)}) collective-permute-start(f32[2,128,1]{2,1,0:T(8,128)S(1)} %get-tuple-element.80), channel_id=1, source_target_pairs={{2,0},{4,2},{6,4},{8,6},{10,8},{12,10},{14,12},{16,14},{18,16},{20... | collective-permute-start | bytes 3080 | tf_op jit(solution)/shard_map/ppermute | solution.py:26
  8.6 4.8 %collective-permute-start.10 = (f32[128,1]{1,0:T(8,128)S(1)}, f32[128,1]{1,0:T(8,128)S(1)}, u32[]{:S(2)}, u32[]{:S(2)}) collective-permute-start(f32[128,1]{1,0:T(8,128)S(1)} %get-tuple-element.94), channel_id=1, source_target_pairs={{2,0},{4,2},{6,4},{8,6},{10,8},{12,10},{14,12},{16,14},{18,16},{20... | collective-permute-start | bytes 1544 | tf_op jit(solution)/shard_map/ppermute | solution.py:26
  9.3 6.4 %collective-permute-start.9 = (f32[128,1]{1,0:T(8,128)S(1)}, f32[128,1]{1,0:T(8,128)S(1)}, u32[]{:S(2)}, u32[]{:S(2)}) collective-permute-start(f32[128,1]{1,0:T(8,128)S(1)} %get-tuple-element.93), channel_id=1, source_target_pairs={{0,2},{2,4},{4,6},{6,8},{8,10},{10,12},{12,14},{14,16},{16,18},{18... | collective-permute-start | bytes 1544 | tf_op jit(solution)/shard_map/ppermute | solution.py:23
  11.3 6.5 %collective-permute-start.7 = (f32[2,1,130]{2,1,0:T(1,128)S(1)}, f32[2,1,130]{2,1,0:T(1,128)S(1)}, u32[]{:S(2)}, u32[]{:S(2)}) collective-permute-start(f32[2,1,130]{2,1,0:T(1,128)S(1)} %get-tuple-element.61), channel_id=1, source_target_pairs={{0,1},{1,0},{2,3},{3,2},{4,5},{5,4},{6,7},{7,6},{8,9},{9,8},{10,11... | collective-permute-start | bytes 3128 | tf_op jit(solution)/shard_map/ppermute | solution.py:23
  13.3 4.5 %collective-permute-start.8 = (f32[2,1,130]{2,1,0:T(1,128)S(1)}, f32[2,1,130]{2,1,0:T(1,128)S(1)}, u32[]{:S(2)}, u32[]{:S(2)}) collective-permute-start(f32[2,1,130]{2,1,0:T(1,128)S(1)} %get-tuple-element.62), channel_id=1, source_target_pairs={{1,0},{0,1},{3,2},{2,3},{5,4},{4,5},{7,6},{6,7},{9,8},{8,9},{11,10... | collective-permute-start | bytes 3128 | tf_op jit(solution)/shard_map/ppermute | solution.py:26
  15.8 3.6 collective-permute-start.11
  17.3 3.6 collective-permute-start.12
  18.0 99.1 %copy-start.7 = (s32[8,128,128]{2,1,0:T(8,128)S(1)}, s32[8,128,128]{2,1,0:T(8,128)}, u32[]{:S(2)}) copy-start(s32[8,128,128]{2,1,0:T(8,128)} %param.16) | copy-start | bytes 1572868
  18.0 99.1 %copy-start.9 = (f32[8,128,128]{2,1,0:T(8,128)S(1)}, f32[8,128,128]{2,1,0:T(8,128)}, u32[]{:S(2)}) copy-start(f32[8,128,128]{2,1,0:T(8,128)} %param.9) | copy-start | bytes 1572868
  58.8 62.4 %copy-start = (f32[8,128,128]{2,1,0:T(8,128)S(1)}, f32[8,128,128]{2,1,0:T(8,128)}, u32[]{:S(2)}) copy-start(f32[8,128,128]{2,1,0:T(8,128)} %param.12) | copy-start | bytes 1572868
  58.8 62.4 %copy-start.2 = (f32[8,128,128]{2,1,0:T(8,128)S(1)}, f32[8,128,128]{2,1,0:T(8,128)}, u32[]{:S(2)}) copy-start(f32[8,128,128]{2,1,0:T(8,128)} %param.11) | copy-start | bytes 1572868
  58.8 6.4 %collective-permute-start.13 = (f32[128,1]{1,0:T(8,128)S(1)}, f32[128,1]{1,0:T(8,128)S(1)}, u32[]{:S(2)}, u32[]{:S(2)}) collective-permute-start(f32[128,1]{1,0:T(8,128)S(1)} %get-tuple-element.91), channel_id=1, source_target_pairs={{0,2},{2,4},{4,6},{6,8},{8,10},{10,12},{12,14},{14,16},{16,18},{18... | collective-permute-start | bytes 1544 | tf_op jit(solution)/shard_map/ppermute | solution.py:23
  58.9 6.4 %collective-permute-start.14 = (f32[128,1]{1,0:T(8,128)S(1)}, f32[128,1]{1,0:T(8,128)S(1)}, u32[]{:S(2)}, u32[]{:S(2)}) collective-permute-start(f32[128,1]{1,0:T(8,128)S(1)} %get-tuple-element.92), channel_id=1, source_target_pairs={{2,0},{4,2},{6,4},{8,6},{10,8},{12,10},{14,12},{16,14},{18,16},{20... | collective-permute-start | bytes 1544 | tf_op jit(solution)/shard_map/ppermute | solution.py:26
  65.4 3.6 collective-permute-start.15
  65.9 3.6 collective-permute-start.16
  112.7 6.4 %collective-permute-start.17 = (f32[128,1]{1,0:T(8,128)S(1)}, f32[128,1]{1,0:T(8,128)S(1)}, u32[]{:S(2)}, u32[]{:S(2)}) collective-permute-start(f32[128,1]{1,0:T(8,128)S(1)} %get-tuple-element.89), channel_id=1, source_target_pairs={{0,2},{2,4},{4,6},{6,8},{8,10},{10,12},{12,14},{14,16},{16,18},{18... | collective-permute-start | bytes 1544 | tf_op jit(solution)/shard_map/ppermute | solution.py:23
  112.7 6.4 %collective-permute-start.18 = (f32[128,1]{1,0:T(8,128)S(1)}, f32[128,1]{1,0:T(8,128)S(1)}, u32[]{:S(2)}, u32[]{:S(2)}) collective-permute-start(f32[128,1]{1,0:T(8,128)S(1)} %get-tuple-element.90), channel_id=1, source_target_pairs={{2,0},{4,2},{6,4},{8,6},{10,8},{12,10},{14,12},{16,14},{18,16},{20... | collective-permute-start | bytes 1544 | tf_op jit(solution)/shard_map/ppermute | solution.py:26
  119.2 3.6 collective-permute-start.19
  120.7 3.6 collective-permute-start.20
  167.2 13.6 %collective-permute-start.21 = (f32[128,1]{1,0:T(8,128)}, f32[128,1]{1,0:T(8,128)S(1)}, u32[]{:S(2)}, u32[]{:S(2)}) collective-permute-start(f32[128,1]{1,0:T(8,128)} %get-tuple-element.87), channel_id=1, source_target_pairs={{0,2},{2,4},{4,6},{6,8},{8,10},{10,12},{12,14},{14,16},{16,18},{18... | collective-permute-start | bytes 1544 | tf_op jit(solution)/shard_map/ppermute | solution.py:23
  167.2 13.6 %collective-permute-start.22 = (f32[128,1]{1,0:T(8,128)}, f32[128,1]{1,0:T(8,128)S(1)}, u32[]{:S(2)}, u32[]{:S(2)}) collective-permute-start(f32[128,1]{1,0:T(8,128)} %get-tuple-element.88), channel_id=1, source_target_pairs={{2,0},{4,2},{6,4},{8,6},{10,8},{12,10},{14,12},{16,14},{18,16},{20... | collective-permute-start | bytes 1544 | tf_op jit(solution)/shard_map/ppermute | solution.py:26
  173.9 9.1 %copy-start.15 = (s32[1,1,8]{2,1,0:T(1,128)S(1)}, s32[1,1,8]{2,1,0:T(1,128)}, u32[]{:S(2)}) copy-start(s32[1,1,8]{2,1,0:T(1,128)} %param.15) | copy-start | bytes 100
  175.9 176.7 %collective-permute-start = (f32[3,8,128,1]{2,1,3,0:T(8,128)S(1)}, f32[3,8,128,1]{2,1,3,0:T(8,128)S(1)}, u32[]{:S(2)}, u32[]{:S(2)}) collective-permute-start(f32[3,8,128,1]{2,1,3,0:T(8,128)S(1)} %copy.15), channel_id=1, source_target_pairs={{0,2},{2,4},{4,6},{6,8},{8,10},{10,12},{12,14},{14,16},{16,18},{18... | collective-permute-start | bytes 36872 | tf_op jit(solution)/shard_map/ppermute | solution.py:23
  176.4 176.7 %collective-permute-start.1 = (f32[3,8,128,1]{2,1,3,0:T(8,128)S(1)}, f32[3,8,128,1]{2,1,3,0:T(8,128)}, u32[]{:S(2)}, u32[]{:S(2)}) collective-permute-start(f32[3,8,128,1]{2,1,3,0:T(8,128)S(1)} %copy.16), channel_id=1, source_target_pairs={{2,0},{4,2},{6,4},{8,6},{10,8},{12,10},{14,12},{16,14},{18,16},{20... | collective-permute-start | bytes 36872 | tf_op jit(solution)/shard_map/ppermute | solution.py:26
  180.9 3.6 collective-permute-start.23
  181.4 3.6 collective-permute-start.24
  226.6 6.4 %collective-permute-start.25 = (f32[128,1]{1,0:T(8,128)S(1)}, f32[128,1]{1,0:T(8,128)S(1)}, u32[]{:S(2)}, u32[]{:S(2)}) collective-permute-start(f32[128,1]{1,0:T(8,128)S(1)} %get-tuple-element.85), channel_id=1, source_target_pairs={{0,2},{2,4},{4,6},{6,8},{8,10},{10,12},{12,14},{14,16},{16,18},{18... | collective-permute-start | bytes 1544 | tf_op jit(solution)/shard_map/ppermute | solution.py:23
  226.6 6.4 %collective-permute-start.26 = (f32[128,1]{1,0:T(8,128)S(1)}, f32[128,1]{1,0:T(8,128)S(1)}, u32[]{:S(2)}, u32[]{:S(2)}) collective-permute-start(f32[128,1]{1,0:T(8,128)S(1)} %get-tuple-element.86), channel_id=1, source_target_pairs={{2,0},{4,2},{6,4},{8,6},{10,8},{12,10},{14,12},{16,14},{18,16},{20... | collective-permute-start | bytes 1544 | tf_op jit(solution)/shard_map/ppermute | solution.py:26
  233.0 3.6 collective-permute-start.27
  234.6 3.6 collective-permute-start.28
  280.6 6.5 %collective-permute-start.29 = (f32[128,1]{1,0:T(8,128)S(1)}, f32[128,1]{1,0:T(8,128)S(1)}, u32[]{:S(2)}, u32[]{:S(2)}) collective-permute-start(f32[128,1]{1,0:T(8,128)S(1)} %get-tuple-element.83), channel_id=1, source_target_pairs={{0,2},{2,4},{4,6},{6,8},{8,10},{10,12},{12,14},{14,16},{16,18},{18... | collective-permute-start | bytes 1544 | tf_op jit(solution)/shard_map/ppermute | solution.py:23
  280.6 7.0 %collective-permute-start.30 = (f32[128,1]{1,0:T(8,128)S(1)}, f32[128,1]{1,0:T(8,128)S(1)}, u32[]{:S(2)}, u32[]{:S(2)}) collective-permute-start(f32[128,1]{1,0:T(8,128)S(1)} %get-tuple-element.84), channel_id=1, source_target_pairs={{2,0},{4,2},{6,4},{8,6},{10,8},{12,10},{14,12},{16,14},{18,16},{20... | collective-permute-start | bytes 1544 | tf_op jit(solution)/shard_map/ppermute | solution.py:26
  287.7 3.6 collective-permute-start.31
  288.3 3.6 collective-permute-start.32
  290.9 71.9 %collective-permute-start.4 = (f32[2,8,128,128]{3,2,0,1:T(8,128)}, f32[2,8,128,128]{3,2,0,1:T(8,128)}, u32[]{:S(2)}, u32[]{:S(2)}) collective-permute-start(f32[2,8,128,128]{3,2,0,1:T(8,128)} %select_bitcast_fusion), channel_id=1, source_target_pairs={{0,16},{2,18},{4,20},{6,22},{8,24},{10,26},{12,28},{14,30},{16,0},... | collective-permute-start | bytes 3145736 | tf_op jit(solution)/shard_map/ppermute | solution.py:34
  343.6 6.8 %collective-permute-start.33 = (f32[128,1]{1,0:T(8,128)S(1)}, f32[128,1]{1,0:T(8,128)S(1)}, u32[]{:S(2)}, u32[]{:S(2)}) collective-permute-start(f32[128,1]{1,0:T(8,128)S(1)} %get-tuple-element.81), channel_id=1, source_target_pairs={{0,2},{2,4},{4,6},{6,8},{8,10},{10,12},{12,14},{14,16},{16,18},{18... | collective-permute-start | bytes 1544 | tf_op jit(solution)/shard_map/ppermute | solution.py:23
  346.7 3.7 %collective-permute-start.34 = (f32[128,1]{1,0:T(8,128)S(1)}, f32[128,1]{1,0:T(8,128)S(1)}, u32[]{:S(2)}, u32[]{:S(2)}) collective-permute-start(f32[128,1]{1,0:T(8,128)S(1)} %get-tuple-element.82), channel_id=1, source_target_pairs={{2,0},{4,2},{6,4},{8,6},{10,8},{12,10},{14,12},{16,14},{18,16},{20... | collective-permute-start | bytes 1544 | tf_op jit(solution)/shard_map/ppermute | solution.py:26
  350.5 7.1 %collective-permute-start.35 = (f32[1,130]{1,0:T(1,128)S(1)}, f32[1,130]{1,0:T(1,128)S(1)}, u32[]{:S(2)}, u32[]{:S(2)}) collective-permute-start(f32[1,130]{1,0:T(1,128)S(1)} %get-tuple-element.65), channel_id=1, source_target_pairs={{0,1},{1,0},{2,3},{3,2},{4,5},{5,4},{6,7},{7,6},{8,9},{9,8},{10,11... | collective-permute-start | bytes 1568 | tf_op jit(solution)/shard_map/ppermute | solution.py:23
  351.2 6.4 %collective-permute-start.36 = (f32[1,130]{1,0:T(1,128)S(1)}, f32[1,130]{1,0:T(1,128)S(1)}, u32[]{:S(2)}, u32[]{:S(2)}) collective-permute-start(f32[1,130]{1,0:T(1,128)S(1)} %get-tuple-element.66), channel_id=1, source_target_pairs={{1,0},{0,1},{3,2},{2,3},{5,4},{4,5},{7,6},{6,7},{9,8},{8,9},{11,10... | collective-permute-start | bytes 1568 | tf_op jit(solution)/shard_map/ppermute | solution.py:26
  354.3 5.9 %copy-start.1 = (f32[8,128,128]{2,1,0:T(8,128)S(1)}, f32[8,128,128]{2,1,0:T(8,128)}, u32[]{:S(2)}) copy-start(f32[8,128,128]{2,1,0:T(8,128)} %param.12) | copy-start | bytes 1572868
  354.3 5.9 %copy-start.3 = (f32[8,128,128]{2,1,0:T(8,128)S(1)}, f32[8,128,128]{2,1,0:T(8,128)}, u32[]{:S(2)}) copy-start(f32[8,128,128]{2,1,0:T(8,128)} %param.11) | copy-start | bytes 1572868
  354.3 5.9 %copy-start.5 = (f32[1,8,128,128]{3,2,1,0:T(8,128)S(1)}, f32[1,8,128,128]{3,2,1,0:T(8,128)}, u32[]{:S(2)}) copy-start(f32[1,8,128,128]{3,2,1,0:T(8,128)} %copy-done.4) | copy-start | bytes 1572868
  355.5 3.9 %collective-permute-start.2 = (f32[3,8,1,130]{3,2,1,0:T(1,128)S(1)}, f32[3,8,1,130]{3,2,1,0:T(1,128)S(1)}, u32[]{:S(2)}, u32[]{:S(2)}) collective-permute-start(f32[3,8,1,130]{3,2,1,0:T(1,128)S(1)} %get-tuple-element.52), channel_id=1, source_target_pairs={{0,1},{1,0},{2,3},{3,2},{4,5},{5,4},{6,7},{7,6},{8,9},{9,8},{10,11... | collective-permute-start | bytes 37448 | tf_op jit(solution)/shard_map/ppermute | solution.py:23
  356.2 4.0 %collective-permute-start.3 = (f32[3,8,1,130]{3,2,1,0:T(1,128)S(1)}, f32[3,8,1,130]{3,2,1,0:T(1,128)S(1)}, u32[]{:S(2)}, u32[]{:S(2)}) collective-permute-start(f32[3,8,1,130]{3,2,1,0:T(1,128)S(1)} %get-tuple-element.53), channel_id=1, source_target_pairs={{1,0},{0,1},{3,2},{2,3},{5,4},{4,5},{7,6},{6,7},{9,8},{8,9},{11,10... | collective-permute-start | bytes 37448 | tf_op jit(solution)/shard_map/ppermute | solution.py:26
  (5 other events, 12.1 us)
